TPU v7x, 32 devices: a whole 2x2x4 slice. The times are simulated.
32 devices in a mesh: dev: 8 (over z, x), rep: 4 (over y, core).
Axes of the slice: x: 2, y: 2, z: 4, core: 2. Of those that a mesh axis runs over, the one named last changes fastest.
Arguments:
- emb_table: float32 [32768, 160], P('dev'), may hold values from -6 to 6
- feature_ids: int32 [4096, 4, 8], P(('dev', 'rep')), may hold values from 0 to 8191
- lengths: int32 [4096, 4], P(('dev', 'rep')), may hold values from 1 to 8
- cotangent: float32 [4096, 4, 160], P(('dev', 'rep')), may hold values from -6 to 6
Outputs:
- pooled: float32 [4096, 4, 160], P(('dev', 'rep'))
- row_grads: float32 [32768, 160], P(('dev', 'rep'))
All inputs are finite; a program needn't handle non-finite values.
Results may differ from a plain program's by a relative error of at most 0.00008.
Values sent between devices are 32-bit elements; how exact they have to be, the bound alone decides.
A program may use at most 128 MiB of HBM per device.

v0:
```python
import functools

import jax
import jax.numpy as jnp
from jax import lax
from jax.experimental import pallas as pl
from jax.experimental.pallas import tpu as pltpu
from jax.sharding import PartitionSpec as P

F32, BF16, I32, I16 = jnp.float32, jnp.bfloat16, jnp.int32, jnp.int16
ROW_TILE = 256
INNER = 2


def split_bits(value):
    high = value.astype(BF16)
    low = (value - high.astype(F32)).astype(BF16)
    return high, low


def repeat(count, step):
    if count == 1:
        step(0)
    else:
        lax.fori_loop(0, count, lambda at, _: (step(at), 0)[1], 0)


def kernel(
    n, reps, table_in, ids_in, lens_in, cot_in, pool_in, grads, arrived,
    table, raw, lens, cot, ids, stage, ids_buf, peer_ids, cot_buf, peer_cot, counts, rest, halves, part, part_in,
    scaled, sums, total,
    id_send, id_recv, cot_send, cot_recv, pass_send, far_send, far_recv, far_id_send, far_id_recv,
    part_send, part_recv, pool_send, pool_recv, row_send, row_recv,
):
    features, bag, each = ids.shape
    width, rows_dev = table.shape
    owners = n // features
    outer = reps // INNER
    rows_out = rows_dev // reps
    kept = rows_out * INNER
    me = lax.axis_index("dev")
    rep = lax.axis_index("rep")
    feature = me // owners
    lane = me % owners
    group = rep // INNER
    core = rep % INNER
    first_row = group * kept
    bits = features.bit_length() - 1

    def crossed(step):
        value = feature
        for bit in range(bits):
            value = value + (step // (1 << bit) % 2) * (1 - 2 * (feature // (1 << bit) % 2)) * (1 << bit)
        return value

    def near(step):
        return (me + step) % n

    def beside(side):
        return feature * owners + (lane + side) % owners

    def across(step):
        return crossed(step) * owners + lane

    def source_of(step, side):
        return crossed(step) * owners + (lane + side) % owners

    def far(step):
        return (group + step) % outer * INNER + core

    partner = group * INNER + (core + 1) % INNER

    barrier = pltpu.get_barrier_semaphore()
    for step in range(1, n):
        pl.semaphore_signal(
            barrier, inc=1, device_id={"dev": near(step)}, device_id_type=pl.DeviceIdType.MESH
        )
    for step in range(1, outer):
        pl.semaphore_signal(
            barrier, inc=1, device_id={"rep": far(step)}, device_id_type=pl.DeviceIdType.MESH
        )
    pl.semaphore_signal(
        barrier, inc=1, device_id={"rep": partner}, device_id_type=pl.DeviceIdType.MESH
    )
    staged = [
        pltpu.make_async_copy(src, dst, stage.at[at])
        for at, (src, dst) in enumerate(
            ((ids_in, raw), (lens_in, lens), (cot_in, cot), (table_in, table))
        )
    ]
    for copy in staged:
        copy.start()
    staged[0].wait()
    staged[1].wait()
    slot_index = lax.broadcasted_iota(I32, (bag, each), 0)
    for at in range(features):
        ids[at] = jnp.where(slot_index < lens[at : at + 1], raw[at], -(1 << 20))
    staged[2].wait()
    ids_buf[me] = ids[feature]
    cot_buf[me] = cot[feature]
    pl.semaphore_wait(barrier, n - 1 + outer)

    def remote(src, dst, send, recv, axis, to):
        return pltpu.make_async_remote_copy(
            src_ref=src, dst_ref=dst, send_sem=send, recv_sem=recv,
            device_id={axis: to}, device_id_type=pl.DeviceIdType.MESH,
        )

    def id_copy(peer, source):
        return remote(
            ids.at[peer // owners], ids_buf.at[source],
            id_send.at[peer], id_recv.at[source], "dev", peer,
        )

    def cot_copy(peer, source):
        return remote(
            cot.at[peer // owners], cot_buf.at[source],
            cot_send.at[peer], cot_recv.at[source], "dev", peer,
        )

    def pass_copy(source, side):
        return remote(
            cot_buf.at[source], cot_buf.at[source],
            pass_send.at[source // owners, side], cot_recv.at[source], "dev", beside(side),
        )

    def far_copy(source, step, own=False):
        return remote(
            cot.at[feature] if own else cot_buf.at[source], peer_cot.at[step - 1, source],
            far_send.at[step - 1, source], far_recv.at[step - 1, source], "rep", far(step),
        )

    def far_id_copy(step):
        return remote(
            ids_buf, peer_ids.at[step - 1],
            far_id_send.at[step - 1], far_id_recv.at[step - 1], "rep", far(step),
        )

    def part_copy(source, slot):
        return remote(
            part.at[source], part_in.at[slot], part_send.at[source], part_recv.at[slot],
            "dev", feature * owners + source % owners,
        )

    def pool_copy(source, slot):
        return remote(
            part.at[source], pool_in.at[slot],
            pool_send.at[source // owners], pool_recv.at[slot], "dev", source,
        )

    for step in range(1, n):
        id_copy(near(step), me).start()
    for step in (1, 3, 2) if features == 4 else range(1, features):
        cot_copy(across(step), me).start()
    for side in range(1, owners):
        cot_copy(beside(side), me).start()
    for step in range(1, outer):
        far_copy(me, step, True).start()

    staged[3].wait()

    def split_table(tile):
        at = pl.ds(pl.multiple_of(tile * ROW_TILE, ROW_TILE), ROW_TILE)
        start = (first_row + tile * ROW_TILE) % rows_dev
        high, low = split_bits(table[:, pl.ds(pl.multiple_of(start, ROW_TILE), ROW_TILE)])
        halves[:width, at] = high
        halves[width:, at] = low

    repeat(rows_dev // ROW_TILE, split_table)

    def pass_on(step):
        source = across(step)
        cot_copy(source, source).wait_recv()
        for side in range(1, owners):
            pass_copy(source, side).start()
        for away in range(1, outer):
            far_copy(source, away).start()

    def send_far(step):
        for side in range(1, owners):
            source = source_of(step, side)
            cot_copy(source, source).wait_recv()
            for away in range(1, outer):
                far_copy(source, away).start()

    def slot_keys(blocks, rows):
        slots = jnp.concatenate(blocks, axis=1)
        wide = slots.shape[1]
        local = slots - lane * rows_dev
        turned = local - first_row
        turned = jnp.where(turned < 0, turned + rows_dev, turned)
        inside = (local >= 0) & (local < rows_dev) & (turned < rows)
        keys, times = [], []
        for j in range(bag):
            same = (slots == slots[j : j + 1]).astype(I32)
            count = jnp.sum(same, axis=0, keepdims=True)
            keep = inside[j : j + 1]
            if j:
                keep = keep & (jnp.sum(same[:j], axis=0, keepdims=True) == 0)
            key = jnp.where(keep, turned[j : j + 1], -1)
            keys.append(jnp.broadcast_to(key, (16, wide)).astype(I16))
            times.append(jnp.broadcast_to(count.astype(F32), (16, wide)).astype(BF16))
        return keys, times

    def count_rows(keys, times, start, rows, target, columns):
        wide = keys[0].shape[1]
        row = lax.broadcasted_iota(I32, (16, 128), 0)

        def count_tile(tile):
            at = pl.multiple_of(tile * ROW_TILE, ROW_TILE)
            base = row + (tile * ROW_TILE + start)
            for block in range(ROW_TILE // 16):
                here = (base + 16 * block).astype(I16)
                here = jnp.concatenate([here] * (wide // 128), axis=1)
                found = jnp.zeros((16, wide), BF16)
                for j in range(bag):
                    found = jnp.where(keys[j] == here, times[j], found)
                target[pl.ds(at + 16 * block, 16), columns] = found

        repeat(rows // ROW_TILE, count_tile)

    sides = owners // 2

    def pair_columns(step, pair):
        return pl.ds(pl.multiple_of((step * sides + pair) * 2 * each, 2 * each), 2 * each)

    def wait_ids(step):
        for side in range(owners):
            if step or side:
                source = source_of(step, side)
                id_copy(source, source).wait_recv()

    def count_pair(step, pair):
        blocks = [ids_buf[source_of(step, pair * 2 + half)] for half in range(2)]
        keys, times = slot_keys(blocks, rows_dev)
        columns = pair_columns(step, pair)
        count_rows(keys, times, 0, kept, counts, columns)
        count_rows(keys, times, kept, rows_dev - kept, rest, slice(None))

    def pool_pair(step, pair):
        columns = pair_columns(step, pair)
        both = jnp.dot(halves[:, :kept], counts[:, columns], preferred_element_type=F32)
        both = both + jnp.dot(halves[:, kept:], rest[...], preferred_element_type=F32)
        pool = both[:width] + both[width:]
        for half in range(2):
            side = pair * 2 + half
            source = source_of(step, side)
            part[source] = pool[:, half * each : (half + 1) * each]
            if isinstance(side, int):
                if side:
                    part_copy(source, source // owners * owners + lane).start()
            else:
                @pl.when(side > 0)
                def _():
                    part_copy(source, source // owners * owners + lane).start()

    def pools(step):
        def one(pair):
            count_pair(step, pair)
            pool_pair(step, pair)

        repeat(sides, one)

    def sum_parts(step):
        source = across(step)
        value = part[source]
        for side in range(1, owners):
            slot = source // owners * owners + (lane + side) % owners
            part_copy(source, slot).wait_recv()
            value = value + part_in[slot]
        if step:
            part[source] = value
            pool_copy(source, feature).start()
        else:
            pool_in[feature] = value

    def scale_block(live_ids, block, column):
        live = jnp.sum((live_ids >= 0).astype(F32), axis=0, keepdims=True)
        high, low = split_bits(block * (1.0 / live))
        columns = pl.ds(pl.multiple_of(column * each, each), each)
        scaled[:width, columns] = high
        scaled[width:, columns] = low

    def scale_own(step):
        def one(side):
            source = source_of(step, side)
            scale_block(ids_buf[source], cot_buf[source], step * owners + side)

        repeat(owners, one)

    def scale_far(away, step):
        for side in range(owners):
            source = source_of(step, side)
            far_copy(source, away).wait_recv()
            scale_block(peer_ids[away - 1, source], peer_cot[away - 1, source], away * n + step * owners + side)

    def count_far(away, step):
        def one(pair):
            blocks = [peer_ids[away - 1, source_of(step, pair * 2 + half)] for half in range(2)]
            keys, times = slot_keys(blocks, kept)
            count_rows(keys, times, 0, kept, counts, pair_columns(away * features + step, pair))

        repeat(sides, one)

    def grad_tile(start, low, high):
        rows = pl.ds(pl.multiple_of(start, ROW_TILE), ROW_TILE)
        both = lax.dot_general(
            scaled[:, low:high], counts[rows, low:high], (((1,), (1,)), ((), ())),
            preferred_element_type=F32,
        )
        return both[:width] + both[width:]

    def row_copy(tile):
        at = slice(tile * ROW_TILE, (tile + 1) * ROW_TILE)
        return remote(
            total.at[tile], arrived.at[tile], row_send.at[tile], row_recv.at[tile], "rep", partner,
        )

    wait_ids(0)
    pools(0)
    pass_on(1)
    send_far(0)
    for step in range(1, features):
        wait_ids(step)
    for away in range(1, outer):
        far_id_copy(away).start()
    pools(1)
    pass_on(2)
    send_far(1)
    sum_parts(0)
    pools(2)
    sum_parts(1)
    pass_on(3)
    send_far(2)
    pools(3)
    sum_parts(2)
    send_far(3)
    for step in range(features):
        scale_own(step)
    for away in range(1, outer):
        far_id_copy(away).wait_recv()
        for step in range(features):
            count_far(away, step)
            if step == 1 and away == 1:
                sum_parts(3)
    middle = scaled.shape[1] - 2 * owners * each
    for away in range(1, outer):
        for step in range(features - 2 if away == outer - 1 else features):
            scale_far(away, step)

    def add_early(tile):
        columns = pl.ds(pl.multiple_of(tile * ROW_TILE, ROW_TILE), ROW_TILE)
        sums[:, columns] = grad_tile(tile * ROW_TILE, 0, middle)

    repeat(kept // ROW_TILE, add_early)
    for step in range(features - 2, features):
        scale_far(outer - 1, step)
    tiles = rows_out // ROW_TILE
    for tile in range(tiles):
        start = pl.multiple_of((core + 1) % INNER * rows_out + tile * ROW_TILE, ROW_TILE)
        total[tile] = grad_tile(start, middle, scaled.shape[1]) + sums[:, pl.ds(start, ROW_TILE)]
        row_copy(tile).start()
    for tile in range(tiles):
        start = pl.multiple_of(core * rows_out + tile * ROW_TILE, ROW_TILE)
        grads[tile] = grad_tile(start, middle, scaled.shape[1]) + sums[:, pl.ds(start, ROW_TILE)]
    for step in range(1, features):
        pool_copy(across(step), crossed(step)).wait_recv()
    for tile in range(tiles):
        row_copy(tile).wait_recv()

    for tile in range(tiles):
        row_copy(tile).wait_send()
    for step in range(1, n):
        id_copy(near(step), me).wait_send()
    for side in range(1, owners):
        cot_copy(beside(side), me).wait_send()
    for away in range(1, outer):
        far_id_copy(away).wait_send()
        far_copy(me, away, True).wait_send()
    for step in range(features):
        source = across(step)
        if step:
            cot_copy(source, me).wait_send()
            pool_copy(source, feature).wait_send()
            for away in range(1, outer):
                far_copy(source, away).wait_send()
        for side in range(1, owners):
            if step:
                pass_copy(source, side).wait_send()
            other = source_of(step, side)
            for away in range(1, outer):
                far_copy(other, away).wait_send()
            part_copy(other, crossed(step) * owners + lane).wait_send()


def finish(lens, pool, own, arrived, pooled, grads):
    for at in range(pool.shape[0]):
        pooled[at] = pool[at] * (1.0 / lens[at : at + 1].astype(F32))
    for tile in range(own.shape[0]):
        grads[:, tile * ROW_TILE : (tile + 1) * ROW_TILE] = own[tile] + arrived[tile]


def body(n, reps, emb_table, feature_ids, lengths, cotangent):
    rows_dev, width = emb_table.shape
    each, features, bag = feature_ids.shape
    lens = lengths.T
    owners = n // features
    outer = reps // INNER
    rows_out = rows_dev // reps
    kept = rows_out * INNER
    tiles = rows_out // ROW_TILE
    away = max(outer - 1, 1)
    sem = pltpu.SemaphoreType.DMA
    vmem = pl.BlockSpec(memory_space=pltpu.VMEM)
    pool_shape = jax.ShapeDtypeStruct((features, width, each), F32)
    tile_shape = jax.ShapeDtypeStruct((tiles, width, ROW_TILE), F32)
    pool, own, arrived = pl.pallas_call(
        functools.partial(kernel, n, reps),
        out_shape=(pool_shape, tile_shape, tile_shape),
        in_specs=[pl.BlockSpec(memory_space=pl.ANY)] * 4,
        out_specs=[vmem] * 3,
        scratch_shapes=[
            pltpu.VMEM((width, rows_dev), F32),
            pltpu.VMEM((features, bag, each), I32),
            pltpu.VMEM((features, each), I32),
            pltpu.VMEM((features, width, each), F32),
            pltpu.VMEM((features, bag, each), I32),
            sem((4,)),
            pltpu.VMEM((n, bag, each), I32),
            pltpu.VMEM((away, n, bag, each), I32),
            pltpu.VMEM((n, width, each), F32),
            pltpu.VMEM((away, n, width, each), F32),
            pltpu.VMEM((kept, outer * n * each), BF16),
            pltpu.VMEM((rows_dev - kept, 2 * each), BF16),
            pltpu.VMEM((2 * width, rows_dev), BF16),
            pltpu.VMEM((n, width, each), F32),
            pltpu.VMEM((n, width, each), F32),
            pltpu.VMEM((2 * width, outer * n * each), BF16),
            pltpu.VMEM((width, kept), F32),
            pltpu.VMEM((tiles, width, ROW_TILE), F32),
            sem((n,)), sem((n,)), sem((n,)), sem((n,)), sem((features, owners)),
            sem((away, n)), sem((away, n)), sem((away,)), sem((away,)),
            sem((n,)), sem((n,)), sem((features,)), sem((features,)),
            sem((tiles,)), sem((tiles,)),
        ],
        compiler_params=pltpu.CompilerParams(
            collective_id=0, has_side_effects=True, vmem_limit_bytes=60 * 1024 * 1024
        ),
    )(
        emb_table.T, jnp.transpose(feature_ids, (1, 2, 0)), lens,
        jnp.transpose(cotangent, (1, 2, 0)),
    )
    pooled, grads = pl.pallas_call(
        finish,
        out_shape=(pool_shape, jax.ShapeDtypeStruct((width, rows_out), F32)),
        in_specs=[vmem] * 4,
        out_specs=[vmem] * 2,
    )(lens, pool, own, arrived)
    return jnp.transpose(pooled, (2, 0, 1)), grads.T


def solution(mesh):
    return jax.shard_map(
        functools.partial(body, mesh.shape["dev"], mesh.shape["rep"]),
        mesh=mesh,
        in_specs=(
            P("dev", None),
            P(("dev", "rep"), None, None),
            P(("dev", "rep"), None),
            P(("dev", "rep"), None, None),
        ),
        out_specs=(P(("dev", "rep"), None, None), P(("dev", "rep"), None)),
        check_vma=False,
    )
```

profile of v0, /device:TPU:0, one launch (start us, length us, event | category | flops | bytes accessed | tf_op | source)
XLA Modules:
  0.0 39.0 jit_solution(17552966660924068902)
XLA Ops:
  0.6 35.9 %shard_map.59 = (f32[4,160,128]{2,1,0:T(8,128)}, f32[4,160,256]{2,1,0:T(8,128)}, f32[4,160,256]{2,1,0:T(8,128)}) custom-call(f32[160,4096]{1,0:T(8,128)} %bitcast.6, s32[4,8,128]{2,1,0:T(8,128)} %bitcast.8, s32[4,128]{1,0:T(4,128)} %bitcast.9, f32[4,160,128]{2,1,0:T(8,128)} %bitcast.7), custom_call_target="tpu_custom_call" | custom-call | tf_op jit(solution)/shard_map/pallas_call | solution.py:417
  36.6 2.4 %shard_map.60 = (f32[4,160,128]{2,1,0:T(8,128)}, f32[160,1024]{1,0:T(8,128)}) custom-call(s32[4,128]{1,0:T(4,128)} %bitcast.10, f32[4,160,128]{2,1,0:T(8,128)} %get-tuple-element.7.pool, f32[4,160,256]{2,1,0:T(8,128)} %get-tuple-element.8.own, f32[4,160,256]{2,1,0:T(8,128)} %get-tuple-element.9.arrived), custom_call_target="tpu_custom_call" | custom-call | tf_op jit(solution)/shard_map/pallas_call | solution.py:453
where the time goes:
time: 39.2 us; the launch traced here: 39 us
  Pallas kernels  38.3 us (98%)
  between operations  0.64 us (2%)
    pallas_call x1, Pallas kernels, body(): pl.pallas_call(functools.partial(kernel, n, reps), out_shape=(pool_shape,...  35.9 us
    pallas_call x1, Pallas kernels, body(): pl.pallas_call(finish, out_shape=(pool_shape, jax.ShapeDtypeStruct((width...  2.39 us

commit v1 on v0

--- a/solution.py
+++ b/solution.py
@@ -9,6 +9,7 @@
 
 F32, BF16, I32, I16 = jnp.float32, jnp.bfloat16, jnp.int32, jnp.int16
 ROW_TILE = 256
+BLOCK = 64
 INNER = 2
 
 
@@ -27,10 +28,10 @@
 
 def kernel(
     n, reps, table_in, ids_in, lens_in, cot_in, pool_in, grads, arrived,
-    table, raw, lens, cot, ids, stage, ids_buf, peer_ids, cot_buf, peer_cot, counts, rest, halves, part, part_in,
+    table, raw, lens, cot, ids, stage, ids_buf, peer_ids, cot_buf, peer_cot, halves, part, part_in,
     scaled, sums, total,
     id_send, id_recv, cot_send, cot_recv, pass_send, far_send, far_recv, far_id_send, far_id_recv,
-    part_send, part_recv, pool_send, pool_recv, row_send, row_recv,
+    part_send, part_recv, pool_send, pool_recv, row_send, row_recv, *counted,
 ):
     features, bag, each = ids.shape
     width, rows_dev = table.shape
@@ -45,6 +46,8 @@
     group = rep // INNER
     core = rep % INNER
     first_row = group * kept
+    sides = owners // 2
+    counts, rests = counted[: outer * n // 2], counted[outer * n // 2 :]
     bits = features.bit_length() - 1
 
     def crossed(step):
@@ -202,27 +205,21 @@
             times.append(jnp.broadcast_to(count.astype(F32), (16, wide)).astype(BF16))
         return keys, times
 
-    def count_rows(keys, times, start, rows, target, columns):
+    def count_rows(keys, times, start, rows, target):
         wide = keys[0].shape[1]
+        lanes = wide // 128
         row = lax.broadcasted_iota(I32, (16, 128), 0)
-
-        def count_tile(tile):
-            at = pl.multiple_of(tile * ROW_TILE, ROW_TILE)
-            base = row + (tile * ROW_TILE + start)
-            for block in range(ROW_TILE // 16):
-                here = (base + 16 * block).astype(I16)
-                here = jnp.concatenate([here] * (wide // 128), axis=1)
-                found = jnp.zeros((16, wide), BF16)
-                for j in range(bag):
-                    found = jnp.where(keys[j] == here, times[j], found)
-                target[pl.ds(at + 16 * block, 16), columns] = found
-
-        repeat(rows // ROW_TILE, count_tile)
-
-    sides = owners // 2
-
-    def pair_columns(step, pair):
-        return pl.ds(pl.multiple_of((step * sides + pair) * 2 * each, 2 * each), 2 * each)
+        spread = BLOCK // 16
+        keys = [jnp.concatenate([key] * spread, axis=0) for key in keys]
+        times = [jnp.concatenate([time] * spread, axis=0) for time in times]
+        for block in range(rows // BLOCK):
+            first = start + block * BLOCK
+            here = [(row + (first + 16 * at)).astype(I16) for at in range(spread)]
+            here = jnp.concatenate([jnp.concatenate([one] * lanes, axis=1) for one in here], axis=0)
+            found = jnp.zeros((BLOCK, wide), BF16)
+            for key, time in zip(keys, times):
+                found = jnp.where(key == here, time, found)
+            target[block * BLOCK : (block + 1) * BLOCK, :] = found
 
     def wait_ids(step):
         for side in range(owners):
@@ -230,36 +227,32 @@
                 source = source_of(step, side)
                 id_copy(source, source).wait_recv()
 
+    def pair_at(step, pair, away=0):
+        return (away * features + step) * sides + pair
+
     def count_pair(step, pair):
-        blocks = [ids_buf[source_of(step, pair * 2 + half)] for half in range(2)]
-        keys, times = slot_keys(blocks, rows_dev)
-        columns = pair_columns(step, pair)
-        count_rows(keys, times, 0, kept, counts, columns)
-        count_rows(keys, times, kept, rows_dev - kept, rest, slice(None))
+        at = pair_at(step, pair)
+        keys, times = slot_keys([ids_buf[source_of(step, pair * 2 + half)] for half in range(2)], rows_dev)
+        count_rows(keys, times, 0, kept, counts[at])
+        count_rows(keys, times, kept, rows_dev - kept, rests[at % 2])
 
     def pool_pair(step, pair):
-        columns = pair_columns(step, pair)
-        both = jnp.dot(halves[:, :kept], counts[:, columns], preferred_element_type=F32)
-        both = both + jnp.dot(halves[:, kept:], rest[...], preferred_element_type=F32)
-        pool = both[:width] + both[width:]
+        at = pair_at(step, pair)
+        pool = jnp.dot(halves[:, :kept], counts[at][...], preferred_element_type=F32)
+        pool = pool + jnp.dot(halves[:, kept:], rests[at % 2][...], preferred_element_type=F32)
+        pool = pool[:width] + pool[width:]
         for half in range(2):
             side = pair * 2 + half
             source = source_of(step, side)
             part[source] = pool[:, half * each : (half + 1) * each]
-            if isinstance(side, int):
-                if side:
-                    part_copy(source, source // owners * owners + lane).start()
-            else:
-                @pl.when(side > 0)
-                def _():
-                    part_copy(source, source // owners * owners + lane).start()
-
-    def pools(step):
-        def one(pair):
-            count_pair(step, pair)
-            pool_pair(step, pair)
-
-        repeat(sides, one)
+            if side:
+                part_copy(source, source // owners * owners + lane).start()
+
+    def count_far(step, away=1):
+        for pair in range(sides):
+            blocks = [peer_ids[away - 1, source_of(step, pair * 2 + half)] for half in range(2)]
+            keys, times = slot_keys(blocks, kept)
+            count_rows(keys, times, 0, kept, counts[pair_at(step, pair, away)])
 
     def sum_parts(step):
         source = across(step)
@@ -294,18 +287,11 @@
             far_copy(source, away).wait_recv()
             scale_block(peer_ids[away - 1, source], peer_cot[away - 1, source], away * n + step * owners + side)
 
-    def count_far(away, step):
-        def one(pair):
-            blocks = [peer_ids[away - 1, source_of(step, pair * 2 + half)] for half in range(2)]
-            keys, times = slot_keys(blocks, kept)
-            count_rows(keys, times, 0, kept, counts, pair_columns(away * features + step, pair))
-
-        repeat(sides, one)
-
-    def grad_tile(start, low, high):
-        rows = pl.ds(pl.multiple_of(start, ROW_TILE), ROW_TILE)
+    def grad_rows(start, rows, low, high):
+        at = pl.ds(pl.multiple_of(start, ROW_TILE), rows)
+        held = jnp.concatenate([counts[pair][at, :] for pair in range(low, high)], axis=1)
         both = lax.dot_general(
-            scaled[:, low:high], counts[rows, low:high], (((1,), (1,)), ((), ())),
+            scaled[:, low * 2 * each : high * 2 * each], held, (((1,), (1,)), ((), ())),
             preferred_element_type=F32,
         )
         return both[:width] + both[width:]
@@ -316,53 +302,64 @@
             total.at[tile], arrived.at[tile], row_send.at[tile], row_recv.at[tile], "rep", partner,
         )
 
-    wait_ids(0)
-    pools(0)
-    pass_on(1)
-    send_far(0)
-    for step in range(1, features):
-        wait_ids(step)
-    for away in range(1, outer):
-        far_id_copy(away).start()
-    pools(1)
-    pass_on(2)
-    send_far(1)
-    sum_parts(0)
-    pools(2)
-    sum_parts(1)
-    pass_on(3)
-    send_far(2)
-    pools(3)
-    sum_parts(2)
-    send_far(3)
-    for step in range(features):
-        scale_own(step)
+    order = list(range(1, features)) + [0]
+    last = order[-1]
+    before = None
+    for place, step in enumerate(order):
+        for pair in range(sides):
+            if pair == 0 and place == 0:
+                wait_ids(step)
+            count_pair(step, pair)
+            if before is not None:
+                pool_pair(*before)
+            before = step, pair
+        if place == 0:
+            pass_on(1)
+            send_far(0)
+            for other in order[1:]:
+                wait_ids(other)
+            for away in range(1, outer):
+                far_id_copy(away).start()
+        if place == 2:
+            pass_on(2)
+            send_far(1)
+        if place == features - 1:
+            pass_on(3)
+            sum_parts(1)
+    pool_pair(*before)
     for away in range(1, outer):
         far_id_copy(away).wait_recv()
         for step in range(features):
-            count_far(away, step)
-            if step == 1 and away == 1:
-                sum_parts(3)
-    middle = scaled.shape[1] - 2 * owners * each
+            count_far(step, away)
+            if away == 1 and step == 1:
+                send_far(2)
+                sum_parts(2)
+    for step in range(3):
+        scale_own(step)
+    send_far(3)
+    scale_own(3)
+    sum_parts(3)
     for away in range(1, outer):
         for step in range(features - 2 if away == outer - 1 else features):
             scale_far(away, step)
-
-    def add_early(tile):
-        columns = pl.ds(pl.multiple_of(tile * ROW_TILE, ROW_TILE), ROW_TILE)
-        sums[:, columns] = grad_tile(tile * ROW_TILE, 0, middle)
-
-    repeat(kept // ROW_TILE, add_early)
+    pairs = outer * n // 2
+    middle = pairs - 2 * sides
+    for half in range(2):
+        start = half * rows_out
+        sums[:, start : start + rows_out] = grad_rows(start, rows_out, 0, middle)
     for step in range(features - 2, features):
         scale_far(outer - 1, step)
     tiles = rows_out // ROW_TILE
+    start = pl.multiple_of((core + 1) % INNER * rows_out, ROW_TILE)
+    value = grad_rows(start, rows_out, middle, pairs) + sums[:, pl.ds(start, rows_out)]
     for tile in range(tiles):
-        start = pl.multiple_of((core + 1) % INNER * rows_out + tile * ROW_TILE, ROW_TILE)
-        total[tile] = grad_tile(start, middle, scaled.shape[1]) + sums[:, pl.ds(start, ROW_TILE)]
+        total[tile] = value[:, tile * ROW_TILE : (tile + 1) * ROW_TILE]
         row_copy(tile).start()
+    start = pl.multiple_of(core * rows_out, ROW_TILE)
+    value = grad_rows(start, rows_out, middle, pairs) + sums[:, pl.ds(start, rows_out)]
     for tile in range(tiles):
-        start = pl.multiple_of(core * rows_out + tile * ROW_TILE, ROW_TILE)
-        grads[tile] = grad_tile(start, middle, scaled.shape[1]) + sums[:, pl.ds(start, ROW_TILE)]
+        grads[tile] = value[:, tile * ROW_TILE : (tile + 1) * ROW_TILE]
+    sum_parts(0)
     for step in range(1, features):
         pool_copy(across(step), crossed(step)).wait_recv()
     for tile in range(tiles):
@@ -430,8 +427,6 @@
             pltpu.VMEM((away, n, bag, each), I32),
             pltpu.VMEM((n, width, each), F32),
             pltpu.VMEM((away, n, width, each), F32),
-            pltpu.VMEM((kept, outer * n * each), BF16),
-            pltpu.VMEM((rows_dev - kept, 2 * each), BF16),
             pltpu.VMEM((2 * width, rows_dev), BF16),
             pltpu.VMEM((n, width, each), F32),
             pltpu.VMEM((n, width, each), F32),
@@ -442,7 +437,9 @@
             sem((away, n)), sem((away, n)), sem((away,)), sem((away,)),
             sem((n,)), sem((n,)), sem((features,)), sem((features,)),
             sem((tiles,)), sem((tiles,)),
-        ],
+        ]
+        + [pltpu.VMEM((kept, 2 * each), BF16)] * (outer * n // 2)
+        + [pltpu.VMEM((rows_dev - kept, 2 * each), BF16)] * 2,
         compiler_params=pltpu.CompilerParams(
             collective_id=0, has_side_effects=True, vmem_limit_bytes=60 * 1024 * 1024
         ),

time: 39.2 us -> 35.3 us (0.901)
  Pallas kernels: 38.3 us -> 34.4 us
    pallas_call x1, Pallas kernels: 35.9 us -> 32 us  [body(): pl.pallas_call(functools.partial(kernel, n, reps), out_shape=(pool_shape,...]
where the time goes in v1:
time: 35.3 us; the launch traced here: 35 us
  Pallas kernels  34.4 us (97%)
  between operations  0.64 us (2%)
    pallas_call x1, Pallas kernels, body(): pl.pallas_call(functools.partial(kernel, n, reps), out_shape=(pool_shape,...  32 us
    pallas_call x1, Pallas kernels, body(): pl.pallas_call(finish, out_shape=(pool_shape, jax.ShapeDtypeStruct((width...  2.39 us

profile of v1, /device:TPU:0, one launch (start us, length us, event | category | flops | bytes accessed | tf_op | source)
XLA Modules:
  0.0 35.0 jit_solution(8531307133908042249)
XLA Ops:
  0.6 32.0 %shard_map.59 = (f32[4,160,128]{2,1,0:T(8,128)}, f32[4,160,256]{2,1,0:T(8,128)}, f32[4,160,256]{2,1,0:T(8,128)}) custom-call(f32[160,4096]{1,0:T(8,128)} %bitcast.6, s32[4,8,128]{2,1,0:T(8,128)} %bitcast.8, s32[4,128]{1,0:T(4,128)} %bitcast.9, f32[4,160,128]{2,1,0:T(8,128)} %bitcast.7), custom_call_target="tpu_custom_call" | custom-call | tf_op jit(solution)/shard_map/pallas_call | solution.py:414
  32.7 2.4 %shard_map.60 = (f32[4,160,128]{2,1,0:T(8,128)}, f32[160,1024]{1,0:T(8,128)}) custom-call(s32[4,128]{1,0:T(4,128)} %bitcast.10, f32[4,160,128]{2,1,0:T(8,128)} %get-tuple-element.7.pool, f32[4,160,256]{2,1,0:T(8,128)} %get-tuple-element.8.own, f32[4,160,256]{2,1,0:T(8,128)} %get-tuple-element.9.arrived), custom_call_target="tpu_custom_call" | custom-call | tf_op jit(solution)/shard_map/pallas_call | solution.py:450

commit v2 on v1

--- a/solution.py
+++ b/solution.py
@@ -1,4 +1,5 @@
 import functools
+import math
 
 import jax
 import jax.numpy as jnp
@@ -10,6 +11,7 @@
 F32, BF16, I32, I16 = jnp.float32, jnp.bfloat16, jnp.int32, jnp.int16
 ROW_TILE = 256
 BLOCK = 64
+CHUNK = 512
 INNER = 2
 
 
@@ -205,16 +207,16 @@
             times.append(jnp.broadcast_to(count.astype(F32), (16, wide)).astype(BF16))
         return keys, times
 
-    def count_rows(keys, times, start, rows, target):
+    def count_rows(keys, times, start, first, rows, target):
         wide = keys[0].shape[1]
         lanes = wide // 128
         row = lax.broadcasted_iota(I32, (16, 128), 0)
         spread = BLOCK // 16
         keys = [jnp.concatenate([key] * spread, axis=0) for key in keys]
         times = [jnp.concatenate([time] * spread, axis=0) for time in times]
-        for block in range(rows // BLOCK):
-            first = start + block * BLOCK
-            here = [(row + (first + 16 * at)).astype(I16) for at in range(spread)]
+        for block in range(first // BLOCK, (first + rows) // BLOCK):
+            base = start + block * BLOCK
+            here = [(row + (base + 16 * at)).astype(I16) for at in range(spread)]
             here = jnp.concatenate([jnp.concatenate([one] * lanes, axis=1) for one in here], axis=0)
             found = jnp.zeros((BLOCK, wide), BF16)
             for key, time in zip(keys, times):
@@ -230,29 +232,47 @@
     def pair_at(step, pair, away=0):
         return (away * features + step) * sides + pair
 
-    def count_pair(step, pair):
-        at = pair_at(step, pair)
-        keys, times = slot_keys([ids_buf[source_of(step, pair * 2 + half)] for half in range(2)], rows_dev)
-        count_rows(keys, times, 0, kept, counts[at])
-        count_rows(keys, times, kept, rows_dev - kept, rests[at % 2])
-
-    def pool_pair(step, pair):
-        at = pair_at(step, pair)
-        pool = jnp.dot(halves[:, :kept], counts[at][...], preferred_element_type=F32)
-        pool = pool + jnp.dot(halves[:, kept:], rests[at % 2][...], preferred_element_type=F32)
-        pool = pool[:width] + pool[width:]
-        for half in range(2):
-            side = pair * 2 + half
+    def keys_of(step, pair):
+        return slot_keys([ids_buf[source_of(step, pair * 2 + half)] for half in range(2)], rows_dev)
+
+    def halves_of(at):
+        return (counts[at], 0, kept), (rests[at % 2], kept, rows_dev - kept)
+
+    def stage(new, old, whiches=(0, 1)):
+        if new is not None:
+            keys, times = keys_of(*new)
+        pool = None
+        for which in whiches:
+            rows = (kept, rows_dev - kept)[which]
+            for first in range(0, rows, CHUNK):
+                if old is not None:
+                    target, start, _ = halves_of(pair_at(*old))[which]
+                    piece = jnp.dot(
+                        halves[:, start + first : start + first + CHUNK], target[first : first + CHUNK, :],
+                        preferred_element_type=F32,
+                    )
+                    pool = piece if pool is None else pool + piece
+                if new is not None:
+                    target, start, _ = halves_of(pair_at(*new))[which]
+                    count_rows(keys, times, start, first, CHUNK, target)
+        if old is not None:
+            step, pair = old
+            pool = pool[:width] + pool[width:]
+            for half in range(2):
+                source = source_of(step, pair * 2 + half)
+                value = pool[:, half * each : (half + 1) * each]
+                part[source] = value if 0 in whiches else part[source] + value
+
+    def start_parts(step):
+        for side in range(1, owners):
             source = source_of(step, side)
-            part[source] = pool[:, half * each : (half + 1) * each]
-            if side:
-                part_copy(source, source // owners * owners + lane).start()
+            part_copy(source, source // owners * owners + lane).start()
 
     def count_far(step, away=1):
         for pair in range(sides):
             blocks = [peer_ids[away - 1, source_of(step, pair * 2 + half)] for half in range(2)]
             keys, times = slot_keys(blocks, kept)
-            count_rows(keys, times, 0, kept, counts[pair_at(step, pair, away)])
+            count_rows(keys, times, 0, 0, kept, counts[pair_at(step, pair, away)])
 
     def sum_parts(step):
         source = across(step)
@@ -287,14 +307,17 @@
             far_copy(source, away).wait_recv()
             scale_block(peer_ids[away - 1, source], peer_cot[away - 1, source], away * n + step * owners + side)
 
-    def grad_rows(start, rows, low, high):
+    def grad_rows(start, rows, pairs):
         at = pl.ds(pl.multiple_of(start, ROW_TILE), rows)
-        held = jnp.concatenate([counts[pair][at, :] for pair in range(low, high)], axis=1)
+        left = jnp.concatenate([scaled[:, pair * 2 * each : (pair + 1) * 2 * each] for pair in pairs], axis=1)
+        held = jnp.concatenate([counts[pair][at, :] for pair in pairs], axis=1)
         both = lax.dot_general(
-            scaled[:, low * 2 * each : high * 2 * each], held, (((1,), (1,)), ((), ())),
-            preferred_element_type=F32,
+            left, held, (((1,), (1,)), ((), ())), preferred_element_type=F32,
         )
         return both[:width] + both[width:]
+
+    def pairs_of(steps):
+        return [step * sides + pair for step in steps for pair in range(sides)]
 
     def row_copy(tile):
         at = slice(tile * ROW_TILE, (tile + 1) * ROW_TILE)
@@ -302,64 +325,84 @@
             total.at[tile], arrived.at[tile], row_send.at[tile], row_recv.at[tile], "rep", partner,
         )
 
-    order = list(range(1, features)) + [0]
-    last = order[-1]
-    before = None
-    for place, step in enumerate(order):
-        for pair in range(sides):
-            if pair == 0 and place == 0:
-                wait_ids(step)
-            count_pair(step, pair)
-            if before is not None:
-                pool_pair(*before)
-            before = step, pair
-        if place == 0:
-            pass_on(1)
-            send_far(0)
-            for other in order[1:]:
-                wait_ids(other)
-            for away in range(1, outer):
-                far_id_copy(away).start()
-        if place == 2:
-            pass_on(2)
-            send_far(1)
-        if place == features - 1:
-            pass_on(3)
-            sum_parts(1)
-    pool_pair(*before)
+    def alone(work):
+        pl.when(me >= 0)(work)
+
+    def stage_step(new, old, whiches=(0, 1)):
+        if sides == 1:
+            stage(None if new is None else (new, 0), None if old is None else (old, 0), whiches)
+        elif old is not None and 1 in whiches:
+            for pair in range(sides):
+                stage((old, pair), None)
+                stage(None, (old, pair))
+
+    def early_rows(steps, add):
+        groups = [list(steps)] if sides == 1 else [[step] for step in steps]
+        for place, group_steps in enumerate(groups):
+            for half in range(2):
+                rows = slice(half * rows_out, (half + 1) * rows_out)
+                value = grad_rows(half * rows_out, rows_out, pairs_of(group_steps))
+                sums[:, rows] = sums[:, rows] + value if add or place else value
+
+    for step in (1, 2, 3, 0) if sides > 1 else (1,):
+        wait_ids(step)
+    alone(lambda: stage_step(1, None))
+    pass_on(1)
+    send_far(0)
+    for step in (2, 3, 0) if sides == 1 else ():
+        wait_ids(step)
+    for away in range(1, outer):
+        far_id_copy(away).start()
+    alone(lambda: stage_step(2, 1))
+    start_parts(1)
+    alone(lambda: stage_step(3, 2, (0,)))
+    pass_on(2)
+    send_far(1)
+    alone(lambda: stage_step(3, 2, (1,)))
+    start_parts(2)
+    alone(lambda: stage_step(0, 3, (0,)))
+    pass_on(3)
+    alone(lambda: stage_step(0, 3, (1,)))
+    start_parts(3)
+    send_far(2)
+    alone(lambda: stage_step(None, 0))
+    start_parts(0)
     for away in range(1, outer):
         far_id_copy(away).wait_recv()
+    alone(lambda: count_far(0))
+    sum_parts(1)
+    alone(lambda: count_far(1))
+    alone(lambda: count_far(2))
+    send_far(3)
+    sum_parts(2)
+    for step in range(3):
+        scale_own(step)
+    alone(lambda: early_rows((0, 1, 2), False))
+    alone(lambda: count_far(3))
+    sum_parts(3)
+    for away in range(2, outer):
         for step in range(features):
             count_far(step, away)
-            if away == 1 and step == 1:
-                send_far(2)
-                sum_parts(2)
-    for step in range(3):
-        scale_own(step)
-    send_far(3)
+    for away in range(1, outer):
+        for step in range(2 if away == outer - 1 else features):
+            scale_far(away, step)
     scale_own(3)
-    sum_parts(3)
-    for away in range(1, outer):
-        for step in range(features - 2 if away == outer - 1 else features):
-            scale_far(away, step)
-    pairs = outer * n // 2
-    middle = pairs - 2 * sides
-    for half in range(2):
-        start = half * rows_out
-        sums[:, start : start + rows_out] = grad_rows(start, rows_out, 0, middle)
-    for step in range(features - 2, features):
-        scale_far(outer - 1, step)
+    alone(lambda: early_rows(range(3, outer * features - 2), True))
+    scale_far(outer - 1, 2)
+    alone(lambda: early_rows((outer * features - 2,), True))
+    sum_parts(0)
+    scale_far(outer - 1, 3)
+    last = pairs_of((outer * features - 1,))
     tiles = rows_out // ROW_TILE
     start = pl.multiple_of((core + 1) % INNER * rows_out, ROW_TILE)
-    value = grad_rows(start, rows_out, middle, pairs) + sums[:, pl.ds(start, rows_out)]
+    value = grad_rows(start, rows_out, last) + sums[:, pl.ds(start, rows_out)]
     for tile in range(tiles):
         total[tile] = value[:, tile * ROW_TILE : (tile + 1) * ROW_TILE]
         row_copy(tile).start()
     start = pl.multiple_of(core * rows_out, ROW_TILE)
-    value = grad_rows(start, rows_out, middle, pairs) + sums[:, pl.ds(start, rows_out)]
+    value = grad_rows(start, rows_out, last) + sums[:, pl.ds(start, rows_out)]
     for tile in range(tiles):
         grads[tile] = value[:, tile * ROW_TILE : (tile + 1) * ROW_TILE]
-    sum_parts(0)
     for step in range(1, features):
         pool_copy(across(step), crossed(step)).wait_recv()
     for tile in range(tiles):
@@ -411,47 +454,58 @@
     vmem = pl.BlockSpec(memory_space=pltpu.VMEM)
     pool_shape = jax.ShapeDtypeStruct((features, width, each), F32)
     tile_shape = jax.ShapeDtypeStruct((tiles, width, ROW_TILE), F32)
+    scratch = [
+        pltpu.VMEM((width, rows_dev), F32),
+        pltpu.VMEM((features, bag, each), I32),
+        pltpu.VMEM((features, each), I32),
+        pltpu.VMEM((features, width, each), F32),
+        pltpu.VMEM((features, bag, each), I32),
+        sem((4,)),
+        pltpu.VMEM((n, bag, each), I32),
+        pltpu.VMEM((away, n, bag, each), I32),
+        pltpu.VMEM((n, width, each), F32),
+        pltpu.VMEM((away, n, width, each), F32),
+        pltpu.VMEM((2 * width, rows_dev), BF16),
+        pltpu.VMEM((n, width, each), F32),
+        pltpu.VMEM((n, width, each), F32),
+        pltpu.VMEM((2 * width, outer * n * each), BF16),
+        pltpu.VMEM((width, kept), F32),
+        pltpu.VMEM((tiles, width, ROW_TILE), F32),
+        sem((n,)), sem((n,)), sem((n,)), sem((n,)), sem((features, owners)),
+        sem((away, n)), sem((away, n)), sem((away,)), sem((away,)),
+        sem((n,)), sem((n,)), sem((features,)), sem((features,)),
+        sem((tiles,)), sem((tiles,)),
+    ]
+    scratch += [pltpu.VMEM((kept, 2 * each), BF16)] * (outer * n // 2)
+    scratch += [pltpu.VMEM((rows_dev - kept, 2 * each), BF16)] * 2
+    held = [ref for ref in scratch if ref.memory_space == pltpu.VMEM]
+    blocks = sum(math.prod(ref.shape) * jnp.dtype(ref.dtype).itemsize for ref in held)
+    blocks += 4 * (features * width * each + 2 * width * rows_out)
+    limit = min(65000 * 1024, blocks + (12 << 20))
     pool, own, arrived = pl.pallas_call(
         functools.partial(kernel, n, reps),
         out_shape=(pool_shape, tile_shape, tile_shape),
-        in_specs=[pl.BlockSpec(memory_space=pl.ANY)] * 4,
+        in_specs=[pl.BlockSpec(memory_space=pltpu.HBM)] * 4,
         out_specs=[vmem] * 3,
-        scratch_shapes=[
-            pltpu.VMEM((width, rows_dev), F32),
-            pltpu.VMEM((features, bag, each), I32),
-            pltpu.VMEM((features, each), I32),
-            pltpu.VMEM((features, width, each), F32),
-            pltpu.VMEM((features, bag, each), I32),
-            sem((4,)),
-            pltpu.VMEM((n, bag, each), I32),
-            pltpu.VMEM((away, n, bag, each), I32),
-            pltpu.VMEM((n, width, each), F32),
-            pltpu.VMEM((away, n, width, each), F32),
-            pltpu.VMEM((2 * width, rows_dev), BF16),
-            pltpu.VMEM((n, width, each), F32),
-            pltpu.VMEM((n, width, each), F32),
-            pltpu.VMEM((2 * width, outer * n * each), BF16),
-            pltpu.VMEM((width, kept), F32),
-            pltpu.VMEM((tiles, width, ROW_TILE), F32),
-            sem((n,)), sem((n,)), sem((n,)), sem((n,)), sem((features, owners)),
-            sem((away, n)), sem((away, n)), sem((away,)), sem((away,)),
-            sem((n,)), sem((n,)), sem((features,)), sem((features,)),
-            sem((tiles,)), sem((tiles,)),
-        ]
-        + [pltpu.VMEM((kept, 2 * each), BF16)] * (outer * n // 2)
-        + [pltpu.VMEM((rows_dev - kept, 2 * each), BF16)] * 2,
+        scratch_shapes=scratch,
         compiler_params=pltpu.CompilerParams(
-            collective_id=0, has_side_effects=True, vmem_limit_bytes=60 * 1024 * 1024
+            collective_id=0, has_side_effects=True, vmem_limit_bytes=limit
         ),
     )(
-        emb_table.T, jnp.transpose(feature_ids, (1, 2, 0)), lens,
-        jnp.transpose(cotangent, (1, 2, 0)),
+        *(
+            pltpu.with_memory_space_constraint(array, pltpu.HBM)
+            for array in (
+                emb_table.T, jnp.transpose(feature_ids, (1, 2, 0)), lens,
+                jnp.transpose(cotangent, (1, 2, 0)),
+            )
+        )
     )
     pooled, grads = pl.pallas_call(
         finish,
         out_shape=(pool_shape, jax.ShapeDtypeStruct((width, rows_out), F32)),
         in_specs=[vmem] * 4,
         out_specs=[vmem] * 2,
+        compiler_params=pltpu.CompilerParams(vmem_limit_bytes=8 << 20),
     )(lens, pool, own, arrived)
     return jnp.transpose(pooled, (2, 0, 1)), grads.T
 

time: 35.3 us -> 31.2 us (0.88)
  Pallas kernels: 34.4 us -> 30.4 us
    pallas_call x1, Pallas kernels: 32 us -> 29.4 us  [body(): pl.pallas_call(functools.partial(kernel, n, reps), out_shape=(pool_shape,...]
    pallas_call x1, Pallas kernels: 2.39 us -> 1.04 us  [body(): pl.pallas_call(finish, out_shape=(pool_shape, jax.ShapeDtypeStruct((width...]
where the time goes in v2:
time: 31.2 us; the launch traced here: 31.1 us
  Pallas kernels  30.4 us (97%)
  between operations  0.65 us (2%)
    pallas_call x1, Pallas kernels, body(): pl.pallas_call(functools.partial(kernel, n, reps), out_shape=(pool_shape,...  29.4 us
    pallas_call x1, Pallas kernels, body(): pl.pallas_call(finish, out_shape=(pool_shape, jax.ShapeDtypeStruct((width...  1.04 us

profile of v2, /device:TPU:0, one launch (start us, length us, event | category | flops | bytes accessed | tf_op | source)
XLA Modules:
  0.0 31.1 jit_solution(5379468069470867830)
XLA Ops:
  0.6 0.0 copy-start
  0.6 29.4 %shard_map.59 = (f32[4,160,128]{2,1,0:T(8,128)S(1)}, f32[4,160,256]{2,1,0:T(8,128)S(1)}, f32[4,160,256]{2,1,0:T(8,128)S(1)}) custom-call(f32[160,4096]{1,0:T(8,128)} %bitcast.8, s32[4,8,128]{2,1,0:T(8,128)} %bitcast.10, s32[4,128]{1,0:T(4,128)} %bitcast.6, f32[4,160,128]{2,1,0:T(8,128)} %bitcast.9), custom_call_target="tpu_custom_call" | custom-call | tf_op jit(solution)/shard_map/pallas_call | solution.py:485
  30.0 0.0 copy-done
  30.0 1.0 %shard_map.60 = (f32[4,160,128]{2,1,0:T(8,128)}, f32[160,1024]{1,0:T(8,128)}) custom-call(s32[4,128]{1,0:T(4,128)S(1)} %bitcast.7, f32[4,160,128]{2,1,0:T(8,128)S(1)} %get-tuple-element.7.pool, f32[4,160,256]{2,1,0:T(8,128)S(1)} %get-tuple-element.8.own, f32[4,160,256]{2,1,0:T(8,128)S(1)} %get-tuple-element.9.arrived), custom_call_target="tpu_custom_call" | custom-call | tf_op jit(solution)/shard_map/pallas_call | solution.py:503
Async XLA Ops:
  0.6 29.4 %copy-start = (s32[128,4]{0,1:T(4,128)S(1)}, s32[128,4]{0,1:T(4,128)}, u32[]{:S(2)}) copy-start(s32[128,4]{0,1:T(4,128)} %param.6) | copy-start | bytes 6148

commit v3 on v2

--- a/solution.py
+++ b/solution.py
@@ -155,7 +155,7 @@
 
     for step in range(1, n):
         id_copy(near(step), me).start()
-    for step in (1, 3, 2) if features == 4 else range(1, features):
+    for step in (1, 3, 2):
         cot_copy(across(step), me).start()
     for side in range(1, owners):
         cot_copy(beside(side), me).start()
@@ -214,14 +214,22 @@
         spread = BLOCK // 16
         keys = [jnp.concatenate([key] * spread, axis=0) for key in keys]
         times = [jnp.concatenate([time] * spread, axis=0) for time in times]
-        for block in range(first // BLOCK, (first + rows) // BLOCK):
+
+        def count_block(block):
             base = start + block * BLOCK
             here = [(row + (base + 16 * at)).astype(I16) for at in range(spread)]
             here = jnp.concatenate([jnp.concatenate([one] * lanes, axis=1) for one in here], axis=0)
             found = jnp.zeros((BLOCK, wide), BF16)
             for key, time in zip(keys, times):
                 found = jnp.where(key == here, time, found)
-            target[block * BLOCK : (block + 1) * BLOCK, :] = found
+            at = block * BLOCK
+            target[pl.ds(at if sides == 1 else pl.multiple_of(at, BLOCK), BLOCK), :] = found
+
+        if sides == 1:
+            for block in range(first // BLOCK, (first + rows) // BLOCK):
+                count_block(block)
+        else:
+            repeat(rows // BLOCK, lambda block: count_block(first // BLOCK + block))
 
     def wait_ids(step):
         for side in range(owners):
@@ -336,6 +344,22 @@
                 stage((old, pair), None)
                 stage(None, (old, pair))
 
+    def mixed(steps, ahead):
+        if sides > 1:
+            early_rows(steps, False)
+            for step in ahead:
+                count_far(step)
+            return
+        part_rows = kept // 4
+        keyed = [slot_keys([peer_ids[0, source_of(step, half)] for half in range(2)], kept) for step in ahead]
+        for place in range(4):
+            rows = slice(place * part_rows, (place + 1) * part_rows)
+            sums[:, rows] = grad_rows(place * part_rows, part_rows, pairs_of(steps))
+            which = place * len(ahead) // 4
+            rows = kept * len(ahead) // 4
+            target = counts[pair_at(ahead[which], 0, 1)]
+            count_rows(*keyed[which], 0, place * rows - which * kept, rows, target)
+
     def early_rows(steps, add):
         groups = [list(steps)] if sides == 1 else [[step] for step in steps]
         for place, group_steps in enumerate(groups):
@@ -344,7 +368,7 @@
                 value = grad_rows(half * rows_out, rows_out, pairs_of(group_steps))
                 sums[:, rows] = sums[:, rows] + value if add or place else value
 
-    for step in (1, 2, 3, 0) if sides > 1 else (1,):
+    for step in range(features) if sides > 1 else (1,):
         wait_ids(step)
     alone(lambda: stage_step(1, None))
     pass_on(1)
@@ -364,35 +388,32 @@
     pass_on(3)
     alone(lambda: stage_step(0, 3, (1,)))
     start_parts(3)
+    alone(lambda: stage_step(None, 0))
     send_far(2)
-    alone(lambda: stage_step(None, 0))
-    start_parts(0)
     for away in range(1, outer):
         far_id_copy(away).wait_recv()
     alone(lambda: count_far(0))
     sum_parts(1)
     alone(lambda: count_far(1))
+    for step in range(3):
+        scale_own(step)
     alone(lambda: count_far(2))
     send_far(3)
+    start_parts(0)
     sum_parts(2)
-    for step in range(3):
-        scale_own(step)
-    alone(lambda: early_rows((0, 1, 2), False))
-    alone(lambda: count_far(3))
-    sum_parts(3)
+    alone(lambda: mixed((0, 1, 2), (3,)))
     for away in range(2, outer):
         for step in range(features):
             count_far(step, away)
+    sum_parts(3)
     for away in range(1, outer):
         for step in range(2 if away == outer - 1 else features):
             scale_far(away, step)
     scale_own(3)
     alone(lambda: early_rows(range(3, outer * features - 2), True))
     scale_far(outer - 1, 2)
-    alone(lambda: early_rows((outer * features - 2,), True))
-    sum_parts(0)
     scale_far(outer - 1, 3)
-    last = pairs_of((outer * features - 1,))
+    last = pairs_of((outer * features - 2, outer * features - 1))
     tiles = rows_out // ROW_TILE
     start = pl.multiple_of((core + 1) % INNER * rows_out, ROW_TILE)
     value = grad_rows(start, rows_out, last) + sums[:, pl.ds(start, rows_out)]
@@ -403,6 +424,7 @@
     value = grad_rows(start, rows_out, last) + sums[:, pl.ds(start, rows_out)]
     for tile in range(tiles):
         grads[tile] = value[:, tile * ROW_TILE : (tile + 1) * ROW_TILE]
+    sum_parts(0)
     for step in range(1, features):
         pool_copy(across(step), crossed(step)).wait_recv()
     for tile in range(tiles):
@@ -425,9 +447,9 @@
             for away in range(1, outer):
                 far_copy(source, away).wait_send()
         for side in range(1, owners):
+            other = source_of(step, side)
             if step:
                 pass_copy(source, side).wait_send()
-            other = source_of(step, side)
             for away in range(1, outer):
                 far_copy(other, away).wait_send()
             part_copy(other, crossed(step) * owners + lane).wait_send()

time: 31.2 us -> 30.8 us (0.987)
  Pallas kernels: 30.4 us -> 30 us
    pallas_call x1, Pallas kernels: 29.4 us -> 28.9 us  [body(): pl.pallas_call(functools.partial(kernel, n, reps), out_shape=(pool_shape,...]
where the time goes in v3:
time: 30.8 us; the launch traced here: 30.6 us
  Pallas kernels  30 us (97%)
  between operations  0.65 us (2%)
    pallas_call x1, Pallas kernels, body(): pl.pallas_call(functools.partial(kernel, n, reps), out_shape=(pool_shape,...  28.9 us
    pallas_call x1, Pallas kernels, body(): pl.pallas_call(finish, out_shape=(pool_shape, jax.ShapeDtypeStruct((width...  1.04 us

profile of v3, /device:TPU:0, one launch (start us, length us, event | category | flops | bytes accessed | tf_op | source)
XLA Modules:
  0.0 30.6 jit_solution(8423585125967952267)
XLA Ops:
  0.6 0.0 copy-start
  0.6 28.9 %shard_map.59 = (f32[4,160,128]{2,1,0:T(8,128)S(1)}, f32[4,160,256]{2,1,0:T(8,128)S(1)}, f32[4,160,256]{2,1,0:T(8,128)S(1)}) custom-call(f32[160,4096]{1,0:T(8,128)} %bitcast.8, s32[4,8,128]{2,1,0:T(8,128)} %bitcast.10, s32[4,128]{1,0:T(4,128)} %bitcast.6, f32[4,160,128]{2,1,0:T(8,128)} %bitcast.9), custom_call_target="tpu_custom_call" | custom-call | tf_op jit(solution)/shard_map/pallas_call | solution.py:507
  29.6 0.0 copy-done
  29.6 1.0 %shard_map.60 = (f32[4,160,128]{2,1,0:T(8,128)}, f32[160,1024]{1,0:T(8,128)}) custom-call(s32[4,128]{1,0:T(4,128)S(1)} %bitcast.7, f32[4,160,128]{2,1,0:T(8,128)S(1)} %get-tuple-element.7.pool, f32[4,160,256]{2,1,0:T(8,128)S(1)} %get-tuple-element.8.own, f32[4,160,256]{2,1,0:T(8,128)S(1)} %get-tuple-element.9.arrived), custom_call_target="tpu_custom_call" | custom-call | tf_op jit(solution)/shard_map/pallas_call | solution.py:525
Async XLA Ops:
  0.6 29.0 %copy-start = (s32[128,4]{0,1:T(4,128)S(1)}, s32[128,4]{0,1:T(4,128)}, u32[]{:S(2)}) copy-start(s32[128,4]{0,1:T(4,128)} %param.6) | copy-start | bytes 6148
